TPU v7x, 32 devices: a whole 2x2x4 slice. The times are simulated.
32 devices in a mesh: region: 8 (over z, y), sub: 4 (over x, core).
Axes of the slice: x: 2, y: 2, z: 4, core: 2. Of those that a mesh axis runs over, the one named last changes fastest.
Arguments:
- density: bfloat16 [8, 4, 192, 2048], P('region', 'sub'), may hold values from -6 to 6
- inverse: bfloat16 [8, 4, 2048, 2048], P('region', 'sub'), may hold values from -0.125 to 0.125
- projection: bfloat16 [8, 4, 2048, 256], P('region', 'sub'), may hold values from -0.125 to 0.125
- points: float32 [8, 4, 3, 2048], P('region'), may hold values from 0 to 1
- skeleton_points: float32 [8, 4, 3, 256], replicated, may hold values from 0 to 1
- neighbours: int32 [8, 4, 2], P('region', 'sub'), may hold values from 0 to 3, as said below
- reads: int32 [8, 16, 2], replicated, may hold values from 0 to 7, as said below
Outputs:
- result: bfloat16 [8, 4, 192, 2048], P('region', 'sub')
Inputs may be any that keep to these rules, and one draw needn't show every extreme that they name: `neighbours`: each subdomain lists 2 distinct other subdomains of its own region. In reads[g], entries c * 4 to (c + 1) * 4 - 1 have block index // 2 equal to c; their owner regions are distinct and differ from g.
All inputs are finite; a program needn't handle non-finite values.
Results may differ from a plain program's by a relative error of at most 0.0067.
Values may be sent and summed in bfloat16 or wider, within the bound.
A program may use at most 128 MiB of HBM per device.

v0:
```python
import jax
import jax.numpy as jnp
from jax import lax
from jax.sharding import PartitionSpec as P

BLOCK_ROWS = 128
damping = 1.0
softening = 0.05


def kernel(source, target):
    apart_x = source[0][:, None] - target[0][None, :]
    apart_y = source[1][:, None] - target[1][None, :]
    apart_z = source[2][:, None] - target[2][None, :]
    squared = apart_x * apart_x + apart_y * apart_y + apart_z * apart_z
    kernel_tiles = jnp.exp(-damping * jnp.sqrt(squared)) / jnp.sqrt(squared + softening * softening)
    return (kernel_tiles * target.shape[1] ** (-0.5)).astype(jnp.bfloat16)


def per_device(density, inverse, projection, points, skeleton_points, neighbours, reads):
    sub_index = lax.axis_index("sub")
    region_index = lax.axis_index("region")
    groups = lax.axis_size("sub")
    local_rhs = density[0, 0]
    block_inverse = inverse[0, 0]
    rows_rhs = local_rhs.shape[0]
    solved = jnp.dot(local_rhs, block_inverse, preferred_element_type=jnp.float32).astype(
        jnp.bfloat16
    )
    strengths = jnp.dot(solved, projection[0, 0], preferred_element_type=jnp.float32).astype(
        jnp.bfloat16
    )
    region_points = points[0]
    own_points = lax.dynamic_index_in_dim(region_points, sub_index, 0, keepdims=False)
    listed = neighbours[0, 0]
    zeros_field = jnp.zeros(solved.shape, jnp.float32)
    shards = lax.all_gather(solved[None], "sub", axis=0, tiled=True)

    def add_one(offset, running):
        source = lax.dynamic_index_in_dim(shards, offset, 0, keepdims=False)
        mate_points = lax.dynamic_index_in_dim(region_points, offset, 0, keepdims=False)

        def evaluate(total):
            return total + jnp.dot(
                source, kernel(mate_points, own_points), preferred_element_type=jnp.float32
            )

        def unchanged(total):
            return total

        return lax.cond(jnp.any(listed == offset), evaluate, unchanged, running)

    near_field = lax.fori_loop(0, shards.shape[0], add_one, zeros_field)
    block_rows = BLOCK_ROWS
    blocks_each = strengths.shape[1] // block_rows
    per_column = reads.shape[1] // groups
    my_reads = lax.dynamic_index_in_dim(reads, region_index, 0, keepdims=False)
    column_reads = lax.dynamic_slice_in_dim(my_reads, sub_index * per_column, per_column, 0)
    owners = column_reads[:, 0]
    wanted = lax.dynamic_slice_in_dim(reads, sub_index * per_column, per_column, 1)
    matches = wanted[:, :, 0] == region_index
    present = jnp.any(matches, axis=1)
    halves = jnp.sum(jnp.where(matches, wanted[:, :, 1] % blocks_each, 0), axis=1)
    split_blocks = jnp.transpose(strengths.reshape(rows_rhs, blocks_each, block_rows), (1, 0, 2))
    outgoing = jnp.where(
        present[:, None, None], jnp.take(split_blocks, halves, axis=0), jnp.zeros((), jnp.bfloat16)
    )
    arrived = lax.all_to_all(outgoing, "region", split_axis=0, concat_axis=0, tiled=True)
    picked = jnp.take(arrived, owners, axis=0)
    add_shards = lax.all_gather(picked, "sub", axis=0, tiled=True)
    count_rows = add_shards.shape[0]
    group_size = 4

    def add_group(offset, running):
        first_row = offset * group_size
        entries = lax.dynamic_slice_in_dim(my_reads, first_row, group_size, 0)
        group_owners = entries[:, 0]
        group_columns = entries[:, 1] // blocks_each
        group_halves = entries[:, 1] % blocks_each
        located = skeleton_points[group_owners, group_columns].reshape(
            group_size, 3, blocks_each, block_rows
        )
        located = jnp.take_along_axis(located, group_halves[:, None, None, None], axis=2)[:, :, 0]
        sources = jnp.transpose(located, (1, 0, 2)).reshape(3, group_size * block_rows)
        values = lax.dynamic_slice_in_dim(add_shards, first_row, group_size, 0)
        values = jnp.transpose(values, (1, 0, 2)).reshape(rows_rhs, group_size * block_rows)
        return running + jnp.dot(
            values, kernel(sources, own_points), preferred_element_type=jnp.float32
        )

    far_field = lax.fori_loop(0, count_rows // group_size, add_group, zeros_field)
    applied = (local_rhs.astype(jnp.float32) + near_field + far_field).astype(jnp.bfloat16)
    result = jnp.dot(applied, block_inverse, preferred_element_type=jnp.float32).astype(
        jnp.bfloat16
    )
    return result[None, None]


def solution(mesh):
    return jax.shard_map(
        per_device,
        mesh=mesh,
        in_specs=(
            P("region", "sub", None, None),
            P("region", "sub", None, None),
            P("region", "sub", None, None),
            P("region", None, None, None),
            P(),
            P("region", "sub", None),
            P(),
        ),
        out_specs=P("region", "sub", None, None),
        check_vma=False,
    )
```

profile of v0, /device:TPU:0, one launch (start us, length us, event | category | flops | bytes accessed | tf_op | source)
XLA Modules:
  0.0 123.5 jit_solution(12675178542980507038)
XLA Ops:
  6.5 6.4 %fusion.33 = bf16[192,2048]{1,0:T(8,128)(2,1)} fusion(bf16[1,1,2048,2048]{3,2,1,0:T(8,128)(2,1)} %param.14, bf16[1,1,192,2048]{3,2,1,0:T(8,128)(2,1)} %param.13), kind=kOutput, calls=%fused_computation.63 | convolution fusion | flops 1611005952 | bytes 9961472 | tf_op jit(solution)/shard_map/dot_general | solution.py:27
  13.0 0.1 constant_dynamic-slice_fusion.6
  13.1 0.1 copy.30
  13.1 0.3 fusion.53
  13.5 0.1 copy.29
  13.6 1.5 %fusion.42 = bf16[24,2,8,128]{3,2,1,0:T(8,128)(2,1)S(1)} fusion(bf16[192,2048]{1,0:T(8,128)(2,1)} %fusion.33, bf16[1,1,2048,256]{3,2,1,0:T(8,128)(2,1)S(1)} %copy-done), kind=kOutput, calls=%fused_computation.68 | convolution fusion | flops 201375744 | bytes 1933312 | tf_op jit(solution)/shard_map/dot_general | solution.py:30
  15.2 0.6 gather_fusion.2
  15.8 0.9 select_select_fusion
  16.7 7.3 %all-to-all-start = ((bf16[8,192,128]{2,1,0:T(8,128)(2,1)}), bf16[8,192,128]{2,1,0:T(8,128)(2,1)S(1)}, u32[]{:S(2)}, u32[]{:S(2)}) async-start(bf16[8,192,128]{2,1,0:T(8,128)(2,1)} %select_select_fusion), calls=%async_computation | async-start | bytes 786432 | tf_op jit(solution)/shard_map/all_to_all | solution.py:68
  24.1 0.7 copy.47
  24.8 0.7 copy.33
  25.6 10.1 %all-to-all-done = bf16[8,192,128]{2,1,0:T(8,128)(2,1)S(1)} async-done(((bf16[8,192,128]{2,1,0:T(8,128)(2,1)}), bf16[8,192,128]{2,1,0:T(8,128)(2,1)S(1)}, u32[]{:S(2)}, u32[]{:S(2)}) %all-to-all-start) | async-done | bytes 393248 | tf_op jit(solution)/shard_map/all_to_all | solution.py:68
  35.7 0.6 gather_fusion.3
  36.3 0.1 broadcast_select_fusion
  36.4 11.5 %all_gather.7 = bf16[16,192,128]{2,1,0:T(8,128)(2,1)S(1)} all-gather(bf16[4,192,128]{2,1,0:T(8,128)(2,1)S(1)} %broadcast_select_fusion), channel_id=1, replica_groups=mesh['region'=8,'sub'=4] {'sub'}, dimensions={0}, use_global_device_ids=true | all-gather | bytes 983040 | tf_op jit(solution)/shard_map/all_gather | solution.py:70
  47.9 24.9 %while.33 = (s32[]{:T(128)}, f32[192,2048]{1,0:T(8,128)S(1)}, bf16[16,192,128]{2,1,0:T(8,128)(2,1)S(1)}, s32[16,2]{0,1:T(2,128)S(1)}, f32[8,4,3,256]{3,2,1,0:T(4...) while((s32[]{:T(128)}, f32[192,2048]{1,0:T(8,128)S(1)}, ...), condition=%wide.region_8.9_spmd.clone, body=%wide.region_7.8_spmd.clone.sunk | while | flops 417072896 | bytes 4319797 | solution.py:91
  48.0 1.5 %gather_fusion = f32[4,3,256]{2,1,0:T(4,128)S(1)} fusion(f32[8,4,3,256]{3,2,1,0:T(4,128)} %get-tuple-element.545, s32[4]{0:T(128)S(1)} %get-tuple-element.513), kind=kCustom, calls=%fused_computation.clone.clone.1 | custom fusion | bytes 24608 | tf_op jit(solution)/shard_map/while/body/eval_jaxpr/gather | solution.py:80
  49.5 0.6 gather_fusion.1
  50.3 0.2 copy.57
  50.4 3.7 %convolution_add_fusion.2 = f32[192,2048]{1,0:T(8,128)S(1)} fusion(f32[2048]{0:T(1024)S(1)} %bitcast.130, f32[512]{0:T(512)S(1)} %bitcast.136, f32[2048]{0:T(1024)S(1)} %bitcast.131, f32[512]{0:T(512)S(1)} %bitcast.137, f32[2048]{0:T(1024)S(1)} %bitcast.129, f32[512]{0:T(512)S(1)} %bitcast.135, f32[192,2048]{1,0:T(8,128)S(1)} %get-tuple-element.532, ...), kind=kOutput, calls=%fused_computation.18.clone.1 | convolution fusion | flops 417071104 | bytes 3373057 | tf_op jit(solution)/shard_map/while/body/eval_jaxpr/dot_general | solution.py:87
  54.1 0.1 constant_dynamic-slice_fusion.11
  54.3 1.5 %gather_fusion = f32[4,3,256]{2,1,0:T(4,128)S(1)} fusion(f32[8,4,3,256]{3,2,1,0:T(4,128)} %get-tuple-element.545, s32[4]{0:T(128)S(1)} %get-tuple-element.513), kind=kCustom, calls=%fused_computation.clone.clone.1 | custom fusion | bytes 24608 | tf_op jit(solution)/shard_map/while/body/eval_jaxpr/gather | solution.py:80
  55.8 0.6 gather_fusion.1
  56.5 0.2 copy.57
  56.7 3.7 %convolution_add_fusion.2 = f32[192,2048]{1,0:T(8,128)S(1)} fusion(f32[2048]{0:T(1024)S(1)} %bitcast.130, f32[512]{0:T(512)S(1)} %bitcast.136, f32[2048]{0:T(1024)S(1)} %bitcast.131, f32[512]{0:T(512)S(1)} %bitcast.137, f32[2048]{0:T(1024)S(1)} %bitcast.129, f32[512]{0:T(512)S(1)} %bitcast.135, f32[192,2048]{1,0:T(8,128)S(1)} %get-tuple-element.532, ...), kind=kOutput, calls=%fused_computation.18.clone.1 | convolution fusion | flops 417071104 | bytes 3373057 | tf_op jit(solution)/shard_map/while/body/eval_jaxpr/dot_general | solution.py:87
  60.4 0.1 constant_dynamic-slice_fusion.11
  60.5 1.5 %gather_fusion = f32[4,3,256]{2,1,0:T(4,128)S(1)} fusion(f32[8,4,3,256]{3,2,1,0:T(4,128)} %get-tuple-element.545, s32[4]{0:T(128)S(1)} %get-tuple-element.513), kind=kCustom, calls=%fused_computation.clone.clone.1 | custom fusion | bytes 24608 | tf_op jit(solution)/shard_map/while/body/eval_jaxpr/gather | solution.py:80
  62.0 0.6 gather_fusion.1
  62.7 0.2 copy.57
  62.9 3.7 %convolution_add_fusion.2 = f32[192,2048]{1,0:T(8,128)S(1)} fusion(f32[2048]{0:T(1024)S(1)} %bitcast.130, f32[512]{0:T(512)S(1)} %bitcast.136, f32[2048]{0:T(1024)S(1)} %bitcast.131, f32[512]{0:T(512)S(1)} %bitcast.137, f32[2048]{0:T(1024)S(1)} %bitcast.129, f32[512]{0:T(512)S(1)} %bitcast.135, f32[192,2048]{1,0:T(8,128)S(1)} %get-tuple-element.532, ...), kind=kOutput, calls=%fused_computation.18.clone.1 | convolution fusion | flops 417071104 | bytes 3373057 | tf_op jit(solution)/shard_map/while/body/eval_jaxpr/dot_general | solution.py:87
  66.8 1.5 %gather_fusion = f32[4,3,256]{2,1,0:T(4,128)S(1)} fusion(f32[8,4,3,256]{3,2,1,0:T(4,128)} %get-tuple-element.545, s32[4]{0:T(128)S(1)} %get-tuple-element.513), kind=kCustom, calls=%fused_computation.clone.clone.1 | custom fusion | bytes 24608 | tf_op jit(solution)/shard_map/while/body/eval_jaxpr/gather | solution.py:80
  68.3 0.6 gather_fusion.1
  69.0 0.2 copy.57
  69.2 3.7 %convolution_add_fusion.2 = f32[192,2048]{1,0:T(8,128)S(1)} fusion(f32[2048]{0:T(1024)S(1)} %bitcast.130, f32[512]{0:T(512)S(1)} %bitcast.136, f32[2048]{0:T(1024)S(1)} %bitcast.131, f32[512]{0:T(512)S(1)} %bitcast.137, f32[2048]{0:T(1024)S(1)} %bitcast.129, f32[512]{0:T(512)S(1)} %bitcast.135, f32[192,2048]{1,0:T(8,128)S(1)} %get-tuple-element.532, ...), kind=kOutput, calls=%fused_computation.18.clone.1 | convolution fusion | flops 417071104 | bytes 3373057 | tf_op jit(solution)/shard_map/while/body/eval_jaxpr/dot_general | solution.py:87
  72.9 1.1 copy-done.1
  74.0 0.2 broadcast_in_dim.65
  74.2 35.9 %while.32 = (s32[]{:T(128)}, f32[192,2048]{1,0:T(8,128)S(1)}, s32[2]{0:T(128)S(1)}, bf16[4,192,2048]{2,1,0:T(8,128)(2,1)}, f32[4,3,2048]{2,1,0:T(4,128)}, /*index=5*/f32[3,2048]{1,0:T(4,128)S(1)}, s32[]{:T(128)}) while((s32[]{:T(128)}, f32[192,2048]{1,0:T(8,128)S(1)}, s32[2]{0:T(128)S(1)}, bf16[4,192,2048]{2,1,0:T(8,128)(2,1)}, ...), condition=%wide.region_4.5_spmd, body=%wide.region_0.4_spmd.sunk | while | flops 1665531904 | bytes 4080315 | solution.py:53
  74.4 0.7 compare_reduce_fusion.2
  75.7 0.7 compare_reduce_fusion.2
  77.0 15.2 %conditional.2 = (f32[192,2048]{1,0:T(8,128)S(1)}) conditional(s32[]{:T(128)} %convert_element_type.63, f32[192,2048]{1,0:T(8,128)S(1)} %get-tuple-element.559, (s32[]{:T(128)}, bf16[4,192,2048]{2,1,0:T(8,128)(2,1)}, f32[4,3,2048]{2,1,0:T(4,128)}, f32[3,2048]{1,0:T(4,128)S(1)}, f32[192,2048]{1,0:T(8,128)S(1)}) %tuple.98), branch_computations={%region_2.2_spmd, %region_3.3_spmd} | conditional | flops 1665531904 | bytes 4080172 | solution.py:51
  77.0 0.9 constant_dynamic-slice_fusion.1
  77.9 14.3 %fusion.1 = f32[192,2048]{1,0:T(8,128)S(1)} fusion(f32[192,2048]{1,0:T(8,128)S(1)} %get-tuple-element.323, f32[2048]{0:T(1024)S(1)} %bitcast.133, f32[2048]{0:T(1024)S(1)} %bitcast.128, f32[2048]{0:T(1024)S(1)} %bitcast.134, f32[2048]{0:T(1024)S(1)} %bitcast.127, f32[2048]{0:T(1024)S(1)} %bitcast.132, f32[2048]{0:T(1024)S(1)} %bitcast.126, ...), kind=kOutput, calls=%fused_computation.6 | convolution fusion | flops 1665531904 | bytes 3981824 | tf_op jit(solution)/shard_map/while/body/eval_jaxpr/cond/branch_1_fun/dot_general | solution.py:44
  92.2 0.7 compare_reduce_fusion.2
  93.5 15.2 %conditional.2 = (f32[192,2048]{1,0:T(8,128)S(1)}) conditional(s32[]{:T(128)} %convert_element_type.63, f32[192,2048]{1,0:T(8,128)S(1)} %get-tuple-element.559, (s32[]{:T(128)}, bf16[4,192,2048]{2,1,0:T(8,128)(2,1)}, f32[4,3,2048]{2,1,0:T(4,128)}, f32[3,2048]{1,0:T(4,128)S(1)}, f32[192,2048]{1,0:T(8,128)S(1)}) %tuple.98), branch_computations={%region_2.2_spmd, %region_3.3_spmd} | conditional | flops 1665531904 | bytes 4080172 | solution.py:51
  93.5 0.9 constant_dynamic-slice_fusion.1
  94.5 14.3 %fusion.1 = f32[192,2048]{1,0:T(8,128)S(1)} fusion(f32[192,2048]{1,0:T(8,128)S(1)} %get-tuple-element.323, f32[2048]{0:T(1024)S(1)} %bitcast.133, f32[2048]{0:T(1024)S(1)} %bitcast.128, f32[2048]{0:T(1024)S(1)} %bitcast.134, f32[2048]{0:T(1024)S(1)} %bitcast.127, f32[2048]{0:T(1024)S(1)} %bitcast.132, f32[2048]{0:T(1024)S(1)} %bitcast.126, ...), kind=kOutput, calls=%fused_computation.6 | convolution fusion | flops 1665531904 | bytes 3981824 | tf_op jit(solution)/shard_map/while/body/eval_jaxpr/cond/branch_1_fun/dot_general | solution.py:44
  108.8 0.7 compare_reduce_fusion.2
  110.1 6.6 %fusion.39 = bf16[1,1,192,2048]{3,2,1,0:T(8,128)(2,1)} fusion(bf16[1,1,2048,2048]{3,2,1,0:T(8,128)(2,1)} %param.14, f32[192,2048]{1,0:T(8,128)} %copy-done.1, f32[192,2048]{1,0:T(8,128)S(1)} %get-tuple-element.344, bf16[1,1,192,2048]{3,2,1,0:T(8,128)(2,1)S(1)} %copy-done.2), kind=kOutput, calls=%fused_computation.65 | convolution fusion | flops 1612578816 | bytes 13107200 | tf_op jit(solution)/shard_map/dot_general | solution.py:93
  (79 shorter events, 1.3 us)
Async XLA Ops:
  6.5 7.1 %copy-start = (bf16[1,1,2048,256]{3,2,1,0:T(8,128)(2,1)S(1)}, bf16[1,1,2048,256]{3,2,1,0:T(8,128)(2,1)}, u32[]{:S(2)}) copy-start(bf16[1,1,2048,256]{3,2,1,0:T(8,128)(2,1)} %param.15) | copy-start | bytes 3145732
  6.5 6.4 %copy-start.5 = (s32[8,16,2]{1,2,0:T(2,128)S(1)}, s32[8,16,2]{1,2,0:T(2,128)}, u32[]{:S(2)}) copy-start(s32[8,16,2]{1,2,0:T(2,128)} %param.19) | copy-start | bytes 3076
  6.5 66.3 %all-gather.3.cloned.1.call-start = ((), (), s32[]{:S(2)}) async-start(), calls=%async_computation.1 | async-start | bytes 3932160 | tf_op jit(solution)/shard_map/all_gather | solution.py:37
  12.9 11.1 %copy-start.3 = (f32[1,4,3,2048]{3,1,2,0:T(4,128)S(1)}, f32[1,4,3,2048]{3,1,2,0:T(4,128)}, u32[]{:S(2)}) copy-start(f32[1,4,3,2048]{3,1,2,0:T(4,128)} %param.16) | copy-start | bytes 294916
  12.9 11.9 %copy-start.4 = (f32[8,4,3,256]{3,1,2,0:T(4,128)S(1)}, f32[8,4,3,256]{3,1,2,0:T(4,128)}, u32[]{:S(2)}) copy-start(f32[8,4,3,256]{3,1,2,0:T(4,128)} %param.17) | copy-start | bytes 294916
  16.7 19.0 %all-to-all-start = ((bf16[8,192,128]{2,1,0:T(8,128)(2,1)}), bf16[8,192,128]{2,1,0:T(8,128)(2,1)S(1)}, u32[]{:S(2)}, u32[]{:S(2)}) async-start(bf16[8,192,128]{2,1,0:T(8,128)(2,1)} %select_select_fusion), calls=%async_computation | async-start | bytes 786432 | tf_op jit(solution)/shard_map/all_to_all | solution.py:68
  47.9 26.3 %copy-start.6 = (s32[1,1,2]{2,1,0:T(1,128)S(1)}, s32[1,1,2]{2,1,0:T(1,128)}, u32[]{:S(2)}) copy-start(s32[1,1,2]{2,1,0:T(1,128)} %param.18) | copy-start | bytes 28
  72.8 1.2 copy-start.1
  74.2 35.9 %copy-start.2 = (bf16[1,1,192,2048]{3,2,1,0:T(8,128)(2,1)S(1)}, bf16[1,1,192,2048]{3,2,1,0:T(8,128)(2,1)}, u32[]{:S(2)}) copy-start(bf16[1,1,192,2048]{3,2,1,0:T(8,128)(2,1)} %param.13) | copy-start | bytes 2359300
Sparse Core Ops, SparseCore 0:
  13.1 34.1 all-gather.2
where the time goes:
time: 124 us
  matrix products  57.7 us (47%)
  local copies, waits for them, and re-layouts  15.6 us (13%)
  between operations  13.6 us (11%)
  blocking collectives  11.5 us (9%)
  waiting for transfers between devices  10.1 us (8%)
  starting transfers between devices  7.31 us (6%)
  other arithmetic  4.52 us (4%)
  loops' own time  3.2 us (3%)
    dot_general x2, matrix products, evaluate(): jnp.dot(source, kernel(mate_points, own_points), preferred_element_type=j...  28.5 us
    dot_general x4, matrix products, add_group(): jnp.dot(values, kernel(sources, own_points), preferred_element_type=jnp.f...  14.7 us
    all_gather x1, blocking collectives, per_device(): add_shards = lax.all_gather(picked, 'sub', axis=0, tiled=True)  11.5 us
    all_to_all x1, waiting for transfers between devices, per_device(): lax.all_to_all(outgoing, 'region', split_axis=0, concat_axis=0, tiled=True)  10.1 us
    all_to_all x1, starting transfers between devices, per_device(): lax.all_to_all(outgoing, 'region', split_axis=0, concat_axis=0, tiled=True)  7.31 us
    dot_general x1, matrix products, per_device(): jnp.dot(applied, block_inverse, preferred_element_type=jnp.float32)  6.56 us
    dot_general x1, matrix products, per_device(): jnp.dot(local_rhs, block_inverse, preferred_element_type=jnp.float32)  6.4 us
    gather x8, local copies, waits for them, and re-layouts, add_group(): skeleton_points[group_owners, group_columns]  5.96 us
  transfers between devices with their start and end apart: 2, of which 1 were waited for; matrix products, arithmetic and copies ran while one was open for 25% of the time, Pallas kernels for 0%

commit v1 on v0

--- a/solution.py
+++ b/solution.py
@@ -67,7 +67,12 @@
     )
     arrived = lax.all_to_all(outgoing, "region", split_axis=0, concat_axis=0, tiled=True)
     picked = jnp.take(arrived, owners, axis=0)
-    add_shards = lax.all_gather(picked, "sub", axis=0, tiled=True)
+    ring = [picked]
+    for hop in range(3):
+        ring.append(lax.ppermute(ring[-1], "sub", [(dev, (dev + 1) % 4) for dev in range(4)]))
+    add_shards = jnp.roll(
+        jnp.concatenate(ring[::-1], axis=0), (lax.axis_index("sub") + 1) * ring[0].shape[0], axis=0
+    )
     count_rows = add_shards.shape[0]
     group_size = 4
 

time: 124 us -> 130 us (1.048); the launches traced: 124 us -> 128 us
  waiting for transfers between devices: 10.1 us -> 23.6 us
  blocking collectives: 11.5 us -> 0 us
  local copies, waits for them, and re-layouts: 15.6 us -> 19.3 us
  matrix products: 57.7 us -> 55.6 us
    ppermute x0 -> x3, waiting for transfers between devices: none -> 12.7 us  [per_device(): lax.ppermute(ring[-1], 'sub', [(dev, (dev + 1) % 4) for dev in range(4)])]
    all_gather x1 -> x0, blocking collectives: 11.5 us -> none  [per_device(): add_shards = lax.all_gather(picked, 'sub', axis=0, tiled=True)]
    unnamed x17 -> x23, local copies, waits for them, and re-layouts: 2.58 us -> 3.48 us
  transfers between devices with their start and end apart: 2 -> 5, of which waited for: 1 -> 4; matrix products, arithmetic and copies ran while one was open for 25% -> 23% of each run, Pallas kernels for 0% -> 0%
where the time goes in v1:
time: 130 us; the launch traced here: 128 us
  matrix products  55.6 us (43%)
  waiting for transfers between devices  23.6 us (18%)
  local copies, waits for them, and re-layouts  19.3 us (15%)
  between operations  13.7 us (11%)
  starting transfers between devices  7.41 us (6%)
  other arithmetic  5.5 us (4%)
  loops' own time  3.14 us (2%)
    dot_general x2, matrix products, evaluate(): jnp.dot(source, kernel(mate_points, own_points), preferred_element_type=j...  28.5 us
    dot_general x4, matrix products, add_group(): jnp.dot(values, kernel(sources, own_points), preferred_element_type=jnp.f...  14.7 us
    ppermute x3, waiting for transfers between devices, per_device(): lax.ppermute(ring[-1], 'sub', [(dev, (dev + 1) % 4) for dev in range(4)])  12.7 us
    all_to_all x1, waiting for transfers between devices, per_device(): lax.all_to_all(outgoing, 'region', split_axis=0, concat_axis=0, tiled=True)  10.8 us
    all_to_all x1, starting transfers between devices, per_device(): lax.all_to_all(outgoing, 'region', split_axis=0, concat_axis=0, tiled=True)  7.31 us
    dot_general x1, matrix products, per_device(): jnp.dot(applied, block_inverse, preferred_element_type=jnp.float32)  6.56 us
    gather x8, local copies, waits for them, and re-layouts, add_group(): skeleton_points[group_owners, group_columns]  5.96 us
    dot_general x1, matrix products, per_device(): jnp.dot(local_rhs, block_inverse, preferred_element_type=jnp.float32)  5.44 us
  transfers between devices with their start and end apart: 5, of which 4 were waited for; matrix products, arithmetic and copies ran while one was open for 23% of the time, Pallas kernels for 0%

profile of v1, /device:TPU:0, one launch (start us, length us, event | category | flops | bytes accessed | tf_op | source)
XLA Modules:
  0.0 128.2 jit_solution(9125630569446282959)
XLA Ops:
  6.5 0.9 constant_dynamic-slice_fusion.7
  7.5 1.0 fusion.53
  8.7 5.4 %fusion.33 = bf16[192,2048]{1,0:T(8,128)(2,1)S(1)} fusion(bf16[1,1,2048,2048]{3,2,1,0:T(8,128)(2,1)} %param.14, bf16[1,1,192,2048]{3,2,1,0:T(8,128)(2,1)} %param.13), kind=kOutput, calls=%fused_computation.63 | convolution fusion | flops 1611005952 | bytes 9961472 | tf_op jit(solution)/shard_map/dot_general | solution.py:27
  14.2 0.4 fusion.42
  14.6 0.6 gather_fusion.2
  15.2 0.9 select_select_fusion
  16.1 7.3 %all-to-all-start = ((bf16[8,192,128]{2,1,0:T(8,128)(2,1)}), bf16[8,192,128]{2,1,0:T(8,128)(2,1)S(1)}, u32[]{:S(2)}, u32[]{:S(2)}) async-start(bf16[8,192,128]{2,1,0:T(8,128)(2,1)} %select_select_fusion), calls=%async_computation | async-start | bytes 786432 | tf_op jit(solution)/shard_map/all_to_all | solution.py:68
  23.4 0.8 fusion.49
  24.2 10.8 %all-to-all-done = bf16[8,192,128]{2,1,0:T(8,128)(2,1)S(1)} async-done(((bf16[8,192,128]{2,1,0:T(8,128)(2,1)}), bf16[8,192,128]{2,1,0:T(8,128)(2,1)S(1)}, u32[]{:S(2)}, u32[]{:S(2)}) %all-to-all-start) | async-done | bytes 393248 | tf_op jit(solution)/shard_map/all_to_all | solution.py:68
  35.1 0.6 gather_fusion.3
  35.8 5.1 %collective-permute-done = bf16[4,192,128]{2,1,0:T(8,128)(2,1)S(1)} collective-permute-done((bf16[4,192,128]{2,1,0:T(8,128)(2,1)S(1)}, bf16[4,192,128]{2,1,0:T(8,128)(2,1)S(1)}, u32[]{:S(2)}, u32[]{:S(2)}) %collective-permute-start) | collective-permute-done | bytes 196640 | tf_op jit(solution)/shard_map/ppermute | solution.py:72
  40.9 5.1 %collective-permute-done.1 = bf16[4,192,128]{2,1,0:T(8,128)(2,1)S(1)} collective-permute-done((bf16[4,192,128]{2,1,0:T(8,128)(2,1)S(1)}, bf16[4,192,128]{2,1,0:T(8,128)(2,1)S(1)}, u32[]{:S(2)}, u32[]{:S(2)}) %collective-permute-start.1) | collective-permute-done | bytes 196640 | tf_op jit(solution)/shard_map/ppermute | solution.py:72
  46.0 0.6 constant_dynamic-slice_fusion.9
  46.6 0.7 copy.39
  47.3 0.8 copy.41
  48.1 0.7 copy.25
  48.8 0.7 fusion.50
  49.5 2.6 %collective-permute-done.2 = bf16[4,192,128]{2,1,0:T(8,128)(2,1)S(1)} collective-permute-done((bf16[4,192,128]{2,1,0:T(8,128)(2,1)S(1)}, bf16[4,192,128]{2,1,0:T(8,128)(2,1)S(1)}, u32[]{:S(2)}, u32[]{:S(2)}) %collective-permute-start.2) | collective-permute-done | bytes 196640 | tf_op jit(solution)/shard_map/ppermute | solution.py:72
  52.6 25.0 %while.33 = (s32[]{:T(128)}, f32[192,2048]{1,0:T(8,128)S(1)}, bf16[16,192,128]{2,1,0:T(8,128)(2,1)S(1)}, s32[16,2]{0,1:T(2,128)S(1)}, f32[8,4,3,256]{3,2,1,0:T(4...) while((s32[]{:T(128)}, f32[192,2048]{1,0:T(8,128)S(1)}, ...), condition=%wide.region_8.9_spmd.clone, body=%wide.region_7.8_spmd.clone.sunk | while | flops 417072896 | bytes 4319797 | solution.py:96
  52.8 1.5 %gather_fusion = f32[4,3,256]{2,1,0:T(4,128)S(1)} fusion(f32[8,4,3,256]{3,2,1,0:T(4,128)} %get-tuple-element.539, s32[4]{0:T(128)S(1)} %get-tuple-element.507), kind=kCustom, calls=%fused_computation.clone.clone.1 | custom fusion | bytes 24608 | tf_op jit(solution)/shard_map/while/body/eval_jaxpr/gather | solution.py:85
  54.3 0.6 gather_fusion.1
  55.0 0.2 copy.49
  55.2 3.7 %convolution_add_fusion.2 = f32[192,2048]{1,0:T(8,128)S(1)} fusion(f32[2048]{0:T(1024)S(1)} %bitcast.130, f32[512]{0:T(512)S(1)} %bitcast.136, f32[2048]{0:T(1024)S(1)} %bitcast.131, f32[512]{0:T(512)S(1)} %bitcast.137, f32[2048]{0:T(1024)S(1)} %bitcast.129, f32[512]{0:T(512)S(1)} %bitcast.135, f32[192,2048]{1,0:T(8,128)S(1)} %get-tuple-element.526, ...), kind=kOutput, calls=%fused_computation.18.clone.1 | convolution fusion | flops 417071104 | bytes 3373057 | tf_op jit(solution)/shard_map/while/body/eval_jaxpr/dot_general | solution.py:92
  59.0 1.5 %gather_fusion = f32[4,3,256]{2,1,0:T(4,128)S(1)} fusion(f32[8,4,3,256]{3,2,1,0:T(4,128)} %get-tuple-element.539, s32[4]{0:T(128)S(1)} %get-tuple-element.507), kind=kCustom, calls=%fused_computation.clone.clone.1 | custom fusion | bytes 24608 | tf_op jit(solution)/shard_map/while/body/eval_jaxpr/gather | solution.py:85
  60.5 0.6 gather_fusion.1
  61.2 0.2 copy.49
  61.4 3.7 %convolution_add_fusion.2 = f32[192,2048]{1,0:T(8,128)S(1)} fusion(f32[2048]{0:T(1024)S(1)} %bitcast.130, f32[512]{0:T(512)S(1)} %bitcast.136, f32[2048]{0:T(1024)S(1)} %bitcast.131, f32[512]{0:T(512)S(1)} %bitcast.137, f32[2048]{0:T(1024)S(1)} %bitcast.129, f32[512]{0:T(512)S(1)} %bitcast.135, f32[192,2048]{1,0:T(8,128)S(1)} %get-tuple-element.526, ...), kind=kOutput, calls=%fused_computation.18.clone.1 | convolution fusion | flops 417071104 | bytes 3373057 | tf_op jit(solution)/shard_map/while/body/eval_jaxpr/dot_general | solution.py:92
  65.3 1.5 %gather_fusion = f32[4,3,256]{2,1,0:T(4,128)S(1)} fusion(f32[8,4,3,256]{3,2,1,0:T(4,128)} %get-tuple-element.539, s32[4]{0:T(128)S(1)} %get-tuple-element.507), kind=kCustom, calls=%fused_computation.clone.clone.1 | custom fusion | bytes 24608 | tf_op jit(solution)/shard_map/while/body/eval_jaxpr/gather | solution.py:85
  66.8 0.6 gather_fusion.1
  67.5 0.2 copy.49
  67.7 3.7 %convolution_add_fusion.2 = f32[192,2048]{1,0:T(8,128)S(1)} fusion(f32[2048]{0:T(1024)S(1)} %bitcast.130, f32[512]{0:T(512)S(1)} %bitcast.136, f32[2048]{0:T(1024)S(1)} %bitcast.131, f32[512]{0:T(512)S(1)} %bitcast.137, f32[2048]{0:T(1024)S(1)} %bitcast.129, f32[512]{0:T(512)S(1)} %bitcast.135, f32[192,2048]{1,0:T(8,128)S(1)} %get-tuple-element.526, ...), kind=kOutput, calls=%fused_computation.18.clone.1 | convolution fusion | flops 417071104 | bytes 3373057 | tf_op jit(solution)/shard_map/while/body/eval_jaxpr/dot_general | solution.py:92
  71.5 1.5 %gather_fusion = f32[4,3,256]{2,1,0:T(4,128)S(1)} fusion(f32[8,4,3,256]{3,2,1,0:T(4,128)} %get-tuple-element.539, s32[4]{0:T(128)S(1)} %get-tuple-element.507), kind=kCustom, calls=%fused_computation.clone.clone.1 | custom fusion | bytes 24608 | tf_op jit(solution)/shard_map/while/body/eval_jaxpr/gather | solution.py:85
  73.0 0.6 gather_fusion.1
  73.9 3.7 %convolution_add_fusion.2 = f32[192,2048]{1,0:T(8,128)S(1)} fusion(f32[2048]{0:T(1024)S(1)} %bitcast.130, f32[512]{0:T(512)S(1)} %bitcast.136, f32[2048]{0:T(1024)S(1)} %bitcast.131, f32[512]{0:T(512)S(1)} %bitcast.137, f32[2048]{0:T(1024)S(1)} %bitcast.129, f32[512]{0:T(512)S(1)} %bitcast.135, f32[192,2048]{1,0:T(8,128)S(1)} %get-tuple-element.526, ...), kind=kOutput, calls=%fused_computation.18.clone.1 | convolution fusion | flops 417071104 | bytes 3373057 | tf_op jit(solution)/shard_map/while/body/eval_jaxpr/dot_general | solution.py:92
  77.6 1.1 copy-done.2
  78.7 0.2 broadcast_in_dim.65
  78.9 35.8 %while.32 = (s32[]{:T(128)}, f32[192,2048]{1,0:T(8,128)S(1)}, s32[2]{0:T(128)S(1)}, bf16[4,192,2048]{2,1,0:T(8,128)(2,1)}, f32[4,3,2048]{2,1,0:T(4,128)}, /*index=5*/f32[3,2048]{1,0:T(4,128)S(1)}, s32[]{:T(128)}) while((s32[]{:T(128)}, f32[192,2048]{1,0:T(8,128)S(1)}, s32[2]{0:T(128)S(1)}, bf16[4,192,2048]{2,1,0:T(8,128)(2,1)}, ...), condition=%wide.region_4.5_spmd, body=%wide.region_0.4_spmd.sunk | while | flops 1665531904 | bytes 4080315 | solution.py:53
  79.1 0.7 compare_reduce_fusion.2
  80.4 0.7 compare_reduce_fusion.2
  81.7 15.2 %conditional.2 = (f32[192,2048]{1,0:T(8,128)S(1)}) conditional(s32[]{:T(128)} %convert_element_type.63, f32[192,2048]{1,0:T(8,128)S(1)} %get-tuple-element.553, (s32[]{:T(128)}, bf16[4,192,2048]{2,1,0:T(8,128)(2,1)}, f32[4,3,2048]{2,1,0:T(4,128)}, f32[3,2048]{1,0:T(4,128)S(1)}, f32[192,2048]{1,0:T(8,128)S(1)}) %tuple.97), branch_computations={%region_2.2_spmd, %region_3.3_spmd} | conditional | flops 1665531904 | bytes 4080172 | solution.py:51
  81.7 0.9 constant_dynamic-slice_fusion.1
  82.7 14.3 %fusion.1 = f32[192,2048]{1,0:T(8,128)S(1)} fusion(f32[192,2048]{1,0:T(8,128)S(1)} %get-tuple-element.323, f32[2048]{0:T(1024)S(1)} %bitcast.133, f32[2048]{0:T(1024)S(1)} %bitcast.128, f32[2048]{0:T(1024)S(1)} %bitcast.134, f32[2048]{0:T(1024)S(1)} %bitcast.127, f32[2048]{0:T(1024)S(1)} %bitcast.132, f32[2048]{0:T(1024)S(1)} %bitcast.126, ...), kind=kOutput, calls=%fused_computation.6 | convolution fusion | flops 1665531904 | bytes 3981824 | tf_op jit(solution)/shard_map/while/body/eval_jaxpr/cond/branch_1_fun/dot_general | solution.py:44
  97.0 0.7 compare_reduce_fusion.2
  98.2 15.2 %conditional.2 = (f32[192,2048]{1,0:T(8,128)S(1)}) conditional(s32[]{:T(128)} %convert_element_type.63, f32[192,2048]{1,0:T(8,128)S(1)} %get-tuple-element.553, (s32[]{:T(128)}, bf16[4,192,2048]{2,1,0:T(8,128)(2,1)}, f32[4,3,2048]{2,1,0:T(4,128)}, f32[3,2048]{1,0:T(4,128)S(1)}, f32[192,2048]{1,0:T(8,128)S(1)}) %tuple.97), branch_computations={%region_2.2_spmd, %region_3.3_spmd} | conditional | flops 1665531904 | bytes 4080172 | solution.py:51
  98.2 0.9 constant_dynamic-slice_fusion.1
  99.2 14.3 %fusion.1 = f32[192,2048]{1,0:T(8,128)S(1)} fusion(f32[192,2048]{1,0:T(8,128)S(1)} %get-tuple-element.323, f32[2048]{0:T(1024)S(1)} %bitcast.133, f32[2048]{0:T(1024)S(1)} %bitcast.128, f32[2048]{0:T(1024)S(1)} %bitcast.134, f32[2048]{0:T(1024)S(1)} %bitcast.127, f32[2048]{0:T(1024)S(1)} %bitcast.132, f32[2048]{0:T(1024)S(1)} %bitcast.126, ...), kind=kOutput, calls=%fused_computation.6 | convolution fusion | flops 1665531904 | bytes 3981824 | tf_op jit(solution)/shard_map/while/body/eval_jaxpr/cond/branch_1_fun/dot_general | solution.py:44
  113.5 0.7 compare_reduce_fusion.2
  114.8 6.6 %fusion.39 = bf16[1,1,192,2048]{3,2,1,0:T(8,128)(2,1)} fusion(bf16[1,1,2048,2048]{3,2,1,0:T(8,128)(2,1)} %param.14, f32[192,2048]{1,0:T(8,128)} %copy-done.2, f32[192,2048]{1,0:T(8,128)S(1)} %get-tuple-element.344, bf16[1,1,192,2048]{3,2,1,0:T(8,128)(2,1)S(1)} %copy-done.3), kind=kOutput, calls=%fused_computation.65 | convolution fusion | flops 1612578816 | bytes 13107200 | tf_op jit(solution)/shard_map/dot_general | solution.py:98
  (93 shorter events, 2.3 us)
Async XLA Ops:
  6.5 7.6 %copy-start = (bf16[1,1,2048,256]{3,2,1,0:T(8,128)(2,1)S(1)}, bf16[1,1,2048,256]{3,2,1,0:T(8,128)(2,1)}, u32[]{:S(2)}) copy-start(bf16[1,1,2048,256]{3,2,1,0:T(8,128)(2,1)} %param.15) | copy-start | bytes 3145732
  14.1 26.8 %copy-start.1 = (bf16[192,2048]{1,0:T(8,128)(2,1)}, bf16[192,2048]{1,0:T(8,128)(2,1)S(1)}, u32[]{:S(2)}) copy-start(bf16[192,2048]{1,0:T(8,128)(2,1)S(1)} %fusion.33) | copy-start | bytes 2359300
  14.1 31.9 %copy-start.4 = (f32[1,4,3,2048]{3,1,2,0:T(4,128)S(1)}, f32[1,4,3,2048]{3,1,2,0:T(4,128)}, u32[]{:S(2)}) copy-start(f32[1,4,3,2048]{3,1,2,0:T(4,128)} %param.16) | copy-start | bytes 294916
  14.1 33.9 %copy-start.5 = (f32[8,4,3,256]{3,1,2,0:T(4,128)S(1)}, f32[8,4,3,256]{3,1,2,0:T(4,128)}, u32[]{:S(2)}) copy-start(f32[8,4,3,256]{3,1,2,0:T(4,128)} %param.17) | copy-start | bytes 294916
  16.1 19.0 %all-to-all-start = ((bf16[8,192,128]{2,1,0:T(8,128)(2,1)}), bf16[8,192,128]{2,1,0:T(8,128)(2,1)S(1)}, u32[]{:S(2)}, u32[]{:S(2)}) async-start(bf16[8,192,128]{2,1,0:T(8,128)(2,1)} %select_select_fusion), calls=%async_computation | async-start | bytes 786432 | tf_op jit(solution)/shard_map/all_to_all | solution.py:68
  23.4 54.2 %all-gather.3.cloned.1.call-start = ((), (), s32[]{:S(2)}) async-start(), calls=%async_computation.1 | async-start | bytes 3932160 | tf_op jit(solution)/shard_map/all_gather | solution.py:37
  35.7 5.1 %collective-permute-start = (bf16[4,192,128]{2,1,0:T(8,128)(2,1)S(1)}, bf16[4,192,128]{2,1,0:T(8,128)(2,1)S(1)}, u32[]{:S(2)}, u32[]{:S(2)}) collective-permute-start(bf16[4,192,128]{2,1,0:T(8,128)(2,1)S(1)} %broadcast_select_fusion), channel_id=1, source_target_pairs={{0,1},{1,2},{2,3},{3,0},{4,5},{5,6},{6,7},{7,4},{8,9},{9,10},{10,1... | collective-permute-start | bytes 589832 | tf_op jit(solution)/shard_map/ppermute | solution.py:72
  40.9 5.1 %collective-permute-start.1 = (bf16[4,192,128]{2,1,0:T(8,128)(2,1)S(1)}, bf16[4,192,128]{2,1,0:T(8,128)(2,1)S(1)}, u32[]{:S(2)}, u32[]{:S(2)}) collective-permute-start(bf16[4,192,128]{2,1,0:T(8,128)(2,1)S(1)} %collective-permute-done), channel_id=1, source_target_pairs={{0,1},{1,2},{2,3},{3,0},{4,5},{5,6},{6,7},{7,4},{8,9},{9,10},{10,1... | collective-permute-start | bytes 589832 | tf_op jit(solution)/shard_map/ppermute | solution.py:72
  46.0 6.1 %collective-permute-start.2 = (bf16[4,192,128]{2,1,0:T(8,128)(2,1)S(1)}, bf16[4,192,128]{2,1,0:T(8,128)(2,1)S(1)}, u32[]{:S(2)}, u32[]{:S(2)}) collective-permute-start(bf16[4,192,128]{2,1,0:T(8,128)(2,1)S(1)} %collective-permute-done.1), channel_id=1, source_target_pairs={{0,1},{1,2},{2,3},{3,0},{4,5},{5,6},{6,7},{7,4},{8,9},{9,10},{10,1... | collective-permute-start | bytes 589832 | tf_op jit(solution)/shard_map/ppermute | solution.py:72
  52.6 26.3 %copy-start.6 = (s32[1,1,2]{2,1,0:T(1,128)S(1)}, s32[1,1,2]{2,1,0:T(1,128)}, u32[]{:S(2)}) copy-start(s32[1,1,2]{2,1,0:T(1,128)} %param.18) | copy-start | bytes 28
  77.6 1.2 copy-start.2
  78.9 35.9 %copy-start.3 = (bf16[1,1,192,2048]{3,2,1,0:T(8,128)(2,1)S(1)}, bf16[1,1,192,2048]{3,2,1,0:T(8,128)(2,1)}, u32[]{:S(2)}) copy-start(bf16[1,1,192,2048]{3,2,1,0:T(8,128)(2,1)} %param.13) | copy-start | bytes 2359300
Sparse Core Ops, SparseCore 0:
  41.0 28.4 all-gather.2
